TPU v7x, 128 devices: a whole 4x4x4 slice. The times are simulated.
128 devices in a mesh: section: 16 (over x_lo, y, core), tensor: 4 (over z), dp: 2 (over x_hi).
Axes of the slice: x: 4 (x_hi: 2, x_lo: 2; x = x_hi * 2 + x_lo), y: 4, z: 4, core: 2. Of those that a mesh axis runs over, the one named last changes fastest.
Arguments:
- section_up: bfloat16 [16, 4096, 7168], P('section', 'dp', 'tensor'), may hold values from -0.09375 to 0.09375
- section_down: bfloat16 [16, 4096, 7168], P('section', 'dp', 'tensor'), may hold values from -0.0625 to 0.0625
- backup_up: bfloat16 [2, 16, 4, 32, 7168], P('dp', 'section', 'tensor'), may hold values from -0.09375 to 0.09375
- backup_down: bfloat16 [2, 16, 4, 32, 7168], P('dp', 'section', 'tensor'), may hold values from -0.0625 to 0.0625
- norm_gain: float32 [16, 4096], P('section'), may hold values from 0.25 to 1.75
- micro_batches: bfloat16 [16, 64, 4096], P(None, 'dp', 'tensor'), may hold values from -24 to 24
- failed_section: int32 [1], replicated, may hold values from 0 to 1048575
- live_batches: int32 [1], replicated, may hold values from 0 to 589823
Outputs:
- finals: bfloat16 [16, 64, 4096], P('section', 'dp', 'tensor')
Inputs may be any that keep to these rules, and one draw needn't show every extreme that they name: failed_section modulo the number of sections names the failed section. micro-batches 0 to 16 // 2 + (live_batches modulo (16 - 16 // 2 + 1)) - 1 run.
All inputs are finite; a program needn't handle non-finite values.
Results may differ from a plain program's by a relative error of at most 0.03.
Values may be sent and summed in bfloat16 or wider, within the bound.
A program may use at most 192 MiB of HBM per device.

v0:
```python
import jax
import jax.numpy as jnp
from jax import lax
from jax.sharding import PartitionSpec as P


def sent_together(arrays, axis, split_dim, concat_dim, along):
    widths = [a.shape[along] for a in arrays]
    both = jnp.concatenate(arrays, axis=along)
    filled = lax.all_to_all(both, axis, split_axis=split_dim, concat_axis=concat_dim, tiled=True)
    return tuple(jnp.split(filled, [sum(widths[:k]) for k in range(1, len(widths))], axis=along))


def in_one_piece(arrays, axis, dim, along):
    ends, at = ([], 0)
    for a in arrays[:-1]:
        at += a.shape[along]
        ends.append(at)
    both = jnp.concatenate(arrays, axis=along)
    return tuple(jnp.split(lax.all_gather(both, axis, axis=dim, tiled=True), ends, axis=along))


def copy_for_each(x, axis):
    copies = jnp.broadcast_to(x, (lax.axis_size(axis), *x.shape))
    return lax.all_to_all(copies, axis, split_axis=0, concat_axis=0, tiled=True)


def taken_together(x, axis):
    return copy_for_each(x, axis).astype(jnp.float32).sum(axis=0)


def passed_along(block, axis, distance):
    devices = range(lax.axis_size(axis))
    route = [(i - distance, i) for i in devices if i - distance in devices]
    return lax.ppermute(block, axis, route)


def split_up(x, dim, count):
    before, after = (x.shape[:dim], x.shape[dim + 1 :])
    return jnp.moveaxis(x.reshape(*before, count, -1, *after), dim, 0)


def sent_and_summed(x, axis, dim):
    count = lax.axis_size(axis)
    blocks = lax.all_to_all(split_up(x, dim, count), axis, 0, 0, tiled=True)
    return jnp.sum(blocks.astype(jnp.float32), axis=0)


def normalize(full_rows, gain_row):
    values = full_rows.astype(jnp.float32)
    mean_square = jnp.mean(values * values, axis=1, keepdims=True)
    return (values * lax.rsqrt(mean_square + 1e-05) * gain_row).astype(jnp.bfloat16)


def body(
    section_up,
    section_down,
    backup_up,
    backup_down,
    norm_gain,
    micro_batches,
    failed_section,
    live_batches,
):
    pieces = sent_together((backup_up, backup_down), "tensor", 4, 2, 0)
    gathered = in_one_piece((pieces[0], pieces[1]), "section", 1, 0)
    block_width = section_up.shape[2]
    rebuilt_up = gathered[0].reshape(-1, block_width)
    rebuilt_down = gathered[1].reshape(-1, block_width)
    section_number = lax.axis_index("section")
    section_count = lax.axis_size("section")
    is_failed = section_number == failed_section[0] % section_count
    mine_up = jnp.where(is_failed, rebuilt_up, section_up[0])
    mine_down = jnp.where(is_failed, rebuilt_down, section_down[0])
    gain_row = norm_gain[0]
    batch_count = micro_batches.shape[0]
    tok_rows = micro_batches.shape[1]
    share_width = micro_batches.shape[2]
    live_count = batch_count // 2 + live_batches[0] % (batch_count - batch_count // 2 + 1)
    tick_total = batch_count + section_count - 1
    full_up, full_down = (
        lax.all_gather(mine_up, "dp", axis=0, tiled=True),
        lax.all_gather(mine_down, "dp", axis=0, tiled=True),
    )

    def section_terms(full_rows, active):

        def compute(rows):
            normed = normalize(rows, gain_row)
            hidden = jax.nn.silu(
                jnp.dot(normed, full_up, preferred_element_type=jnp.float32)
            ).astype(jnp.bfloat16)
            return lax.dot_general(
                hidden, full_down, (((1,), (1,)), ((), ())), preferred_element_type=jnp.float32
            )

        def nothing(rows):
            return jnp.zeros((tok_rows, rows.shape[1]), jnp.float32)

        return lax.cond(active, compute, nothing, full_rows)

    def branch_terms(tick_index, full_rows):
        active = (tick_index >= section_number) & (tick_index - section_number < live_count)
        return section_terms(full_rows, active)

    def entering(source, tick_index):
        picked = lax.dynamic_index_in_dim(
            source, jnp.minimum(tick_index, batch_count - 1), 0, keepdims=False
        )
        return jnp.where(tick_index < live_count, picked, jnp.zeros_like(picked))

    def collect(collected, out_share, tick_index):
        finished = tick_index - (section_count - 1)
        slot_index = jnp.clip(finished, 0, batch_count - 1)
        is_valid = (section_number == section_count - 1) & (finished >= 0)
        previous = lax.dynamic_index_in_dim(collected, slot_index, 0, keepdims=False)
        return lax.dynamic_update_index_in_dim(
            collected, jnp.where(is_valid, out_share, previous), slot_index, 0
        )

    empty_store = jnp.zeros(micro_batches.shape, jnp.bfloat16)
    whole_inputs = lax.all_gather(micro_batches, "tensor", axis=2, tiled=True)
    tensor_number = lax.axis_index("tensor")

    def tick_whole(tick_index, loop_state):
        state_rows, collected = loop_state
        full_rows = jnp.where(section_number == 0, entering(whole_inputs, tick_index), state_rows)
        summed = taken_together(
            branch_terms(tick_index, full_rows).astype(jnp.bfloat16), "tensor"
        ).astype(jnp.float32)
        out_rows = (full_rows.astype(jnp.float32) + summed).astype(jnp.bfloat16)
        out_share = lax.dynamic_slice_in_dim(out_rows, tensor_number * share_width, share_width, 1)
        collected = collect(collected, out_share, tick_index)
        moved = passed_along(out_rows, "section", 1)
        return (moved, collected)

    start_rows = jnp.zeros((tok_rows, whole_inputs.shape[2]), jnp.bfloat16)
    _, collected = lax.fori_loop(0, tick_total, tick_whole, (start_rows, empty_store))
    finals = sent_and_summed(collected.astype(jnp.float32).astype(jnp.bfloat16), "section", 0)
    return finals.astype(jnp.bfloat16)


def solution(mesh):
    placed = (
        P("section", "dp", "tensor"),
        P("section", "dp", "tensor"),
        P("dp", "section", "tensor", None, None),
        P("dp", "section", "tensor", None, None),
        P("section", None),
        P(None, "dp", "tensor"),
        P(),
        P(),
    )
    return jax.shard_map(
        body, mesh=mesh, in_specs=placed, out_specs=P("section", "dp", "tensor"), check_vma=False
    )
```

profile of v0, /device:TPU:63, one launch (start us, length us, event | category | flops | bytes accessed | tf_op | source)
XLA Modules:
  0.0 1675.5 jit_solution(733432057117367775)
XLA Ops:
  19.0 16.3 all_to_all.33
  50.5 81.4 %all-gather.7.cloned.1.call-done = bf16[2,16,4,32,1792]{4,2,3,1,0:T(4,128)(2,1)} async-done(((bf16[2,1,4,32,1792]{4,2,3,1,0:T(4,128)(2,1)}), bf16[2,16,4,32,1792]{4,2,3,1,0:T(4,128)(2,1)}) %all-gather.7.cloned.1.call-update) | async-done | bytes 14680080 | tf_op jit(solution)/shard_map/all_gather | solution.py:20
  131.9 13.0 fusion.14
  182.3 180.7 %all-gather.11.cloned.1.call-done = bf16[4096,1792]{1,0:T(8,128)(2,1)} async-done(((bf16[2048,1792]{1,0:T(8,128)(2,1)}), bf16[4096,1792]{1,0:T(8,128)(2,1)}) %all-gather.11.cloned.1.call-update) | async-done | bytes 14680080 | tf_op jit(solution)/shard_map/all_gather | solution.py:83
  363.0 180.5 %all-gather.9.cloned.1.call-done = bf16[4096,1792]{1,0:T(8,128)(2,1)} async-done(((bf16[2048,1792]{1,0:T(8,128)(2,1)}), bf16[4096,1792]{1,0:T(8,128)(2,1)}) %all-gather.9.cloned.1.call-update) | async-done | bytes 14680080 | tf_op jit(solution)/shard_map/all_gather | solution.py:82
  543.7 1101.4 %while.17 = (s32[]{:T(128)}, bf16[32,4096]{1,0:T(8,128)(2,1)S(1)}, bf16[16,32,1024]{2,1,0:T(8,128)(2,1)S(1)}, pred[]{:T(512)}, s32[]{:T(128)}, /*index=5*/bf16[1...) while((s32[]{:T(128)}, bf16[32,4096]{1,0:T(8,128)(2,1)S(1)}, ...), condition=%wide.region_5.6_spmd, body=%wide.region_0.5_spmd.sunk | while | flops 942333952 | bytes 39404460 | solution.py:138
  550.2 12.9 all-to-all-done
  908.9 152.8 %collective-permute-done = bf16[32,4096]{1,0:T(8,128)(2,1)S(1)} collective-permute-done((bf16[32,4096]{1,0:T(8,128)(2,1)S(1)}, bf16[32,4096]{1,0:T(8,128)(2,1)S(1)}, u32[]{:S(2)}, u32[]{:S(2)}) %collective-permute-start) | collective-permute-done | bytes 262176 | tf_op jit(solution)/shard_map/while/body/eval_jaxpr/ppermute | solution.py:35
  1062.7 13.1 conditional.2
  1062.9 12.9 fusion.10
  1091.8 9.6 collective-permute-done
  1102.4 13.1 conditional.2
  1102.6 12.9 fusion.10
  1131.5 9.6 collective-permute-done
  1142.1 13.1 conditional.2
  1142.3 12.9 fusion.10
  1171.2 9.6 collective-permute-done
  1181.8 13.1 conditional.2
  1182.0 12.9 fusion.10
  1210.9 9.6 collective-permute-done
  1221.5 13.1 conditional.2
  1221.7 12.9 fusion.10
  1250.6 9.6 collective-permute-done
  1261.2 13.1 conditional.2
  1261.4 12.9 fusion.10
  1290.3 9.6 collective-permute-done
  1300.9 13.1 conditional.2
  1301.1 12.9 fusion.10
  1330.0 9.6 collective-permute-done
  1340.6 13.1 conditional.2
  1340.8 12.9 fusion.10
  1369.8 9.6 collective-permute-done
  1380.3 13.1 conditional.2
  1380.5 12.9 fusion.10
  1409.5 9.6 collective-permute-done
  1420.0 13.1 conditional.2
  1420.2 12.9 fusion.10
  1449.2 9.6 collective-permute-done
  1459.8 13.1 conditional.2
  1460.0 12.9 fusion.10
  1488.9 9.6 collective-permute-done
  1499.5 13.1 conditional.2
  1499.7 12.9 fusion.10
  1528.6 9.6 collective-permute-done
  1539.2 13.1 conditional.2
  1539.4 12.9 fusion.10
  1577.2 13.9 all-to-all-done
  1645.0 23.1 %all_to_all.34 = bf16[16,1,32,1024]{3,2,1,0:T(8,128)(2,1)S(1)} all-to-all(bf16[16,1,32,1024]{3,2,1,0:T(8,128)(2,1)S(1)} %bitcast.42), channel_id=1, replica_groups=mesh['section'=16,'tensor'=4,'dp'=2] {'section'}, dimensions={0} | all-to-all | bytes 2097152 | tf_op jit(solution)/shard_map/all_to_all | solution.py:45
  (382 shorter events, 701.2 us)
Async XLA Ops:
  6.5 125.4 %all-gather.7.cloned.1.call-start = ((), (), s32[]{:S(2)}) async-start(), calls=%async_computation.4 | async-start | bytes 15597568 | tf_op jit(solution)/shard_map/all_gather | solution.py:20
  49.1 133.2 %all-gather.5.cloned.1.call-start = ((), (), s32[]{:S(2)}) async-start(), calls=%async_computation.3 | async-start | bytes 5242880 | tf_op jit(solution)/shard_map/all_gather | solution.py:122
  49.8 313.2 %all-gather.11.cloned.1.call-start = ((), (), s32[]{:S(2)}) async-start(), calls=%async_computation.6 | async-start | bytes 22020096 | tf_op jit(solution)/shard_map/all_gather | solution.py:83
  158.4 385.1 %all-gather.9.cloned.1.call-start = ((), (), s32[]{:S(2)}) async-start(), calls=%async_computation.5 | async-start | bytes 22020096 | tf_op jit(solution)/shard_map/all_gather | solution.py:82
  545.9 17.2 %all-to-all-start = ((bf16[4,32,4096]{2,1,0:T(8,128)(2,1)}), bf16[4,32,4096]{2,1,0:T(8,128)(2,1)S(1)}, u32[]{:S(2)}, u32[]{:S(2)}) async-start(bf16[4,32,4096]{2,1,0:T(8,128)(2,1)} %broadcast_in_dim.27), calls=%async_computation | async-start | bytes 2097152 | tf_op jit(solution)/shard_map/while/body/eval_jaxpr/all_to_all | solution.py:25
  570.5 13.6 all-to-all-start
  595.4 13.6 all-to-all-start
  620.2 13.6 all-to-all-start
  645.1 13.6 all-to-all-start
  670.0 13.6 all-to-all-start
  694.9 13.6 all-to-all-start
  719.8 13.6 all-to-all-start
  744.7 13.6 all-to-all-start
  769.6 13.6 all-to-all-start
  794.5 13.6 all-to-all-start
  819.4 13.6 all-to-all-start
  844.3 13.6 all-to-all-start
  869.1 13.6 all-to-all-start
  894.0 13.2 all-to-all-start
  907.5 154.2 %collective-permute-start = (bf16[32,4096]{1,0:T(8,128)(2,1)S(1)}, bf16[32,4096]{1,0:T(8,128)(2,1)S(1)}, u32[]{:S(2)}, u32[]{:S(2)}) collective-permute-start(bf16[32,4096]{1,0:T(8,128)(2,1)S(1)} %add_convert_fusion.2), channel_id=1, source_target_pairs={{0,8},{8,16},{16,24},{24,32},{32,40},{40,48},{48,56},{56,64},{64,7... | collective-permute-start | bytes 786440 | tf_op jit(solution)/shard_map/while/body/eval_jaxpr/ppermute | solution.py:35
  1077.0 13.2 all-to-all-start
  1090.4 10.9 collective-permute-start
  1116.7 13.2 all-to-all-start
  1130.1 11.0 collective-permute-start
  1156.4 13.2 all-to-all-start
  1169.8 10.9 collective-permute-start
  1196.1 13.2 all-to-all-start
  1209.6 11.0 collective-permute-start
  1235.8 13.2 all-to-all-start
  1249.3 10.9 collective-permute-start
  1275.5 13.2 all-to-all-start
  1289.0 11.0 collective-permute-start
  1315.2 13.2 all-to-all-start
  1328.7 10.9 collective-permute-start
  1354.9 13.2 all-to-all-start
  1368.4 11.0 collective-permute-start
  1394.7 13.2 all-to-all-start
  1408.1 10.9 collective-permute-start
  1434.4 13.2 all-to-all-start
  1447.8 11.0 collective-permute-start
  1474.1 13.2 all-to-all-start
  1487.5 10.9 collective-permute-start
  1513.8 13.2 all-to-all-start
  1527.2 11.0 collective-permute-start
  1553.5 13.2 all-to-all-start
  1572.6 18.5 %all-to-all-start = ((bf16[4,32,4096]{2,1,0:T(8,128)(2,1)}), bf16[4,32,4096]{2,1,0:T(8,128)(2,1)S(1)}, u32[]{:S(2)}, u32[]{:S(2)}) async-start(bf16[4,32,4096]{2,1,0:T(8,128)(2,1)} %broadcast_in_dim.27), calls=%async_computation | async-start | bytes 2097152 | tf_op jit(solution)/shard_map/while/body/eval_jaxpr/all_to_all | solution.py:25
  1597.5 13.6 all-to-all-start
  1622.4 13.6 all-to-all-start
  (19 other events, 513.4 us)
Sparse Core Ops, SparseCore 0:
  49.2 82.6 all-gather.6
  133.6 48.6 all-gather.4
  184.0 178.9 all-gather.10
  364.5 178.9 all-gather.8
where the time goes:
time: 1670 us; the launch traced here: 1680 us
  waiting for transfers between devices  1120 us (67%)
  starting transfers between devices  184 us (11%)
  matrix products  168 us (10%)
  local copies, waits for them, and re-layouts  85.6 us (5%)
  other arithmetic  61.6 us (4%)
  blocking collectives  39.4 us (2%)
    ppermute x31, waiting for transfers between devices, passed_along(): return lax.ppermute(block, axis, route)  388 us
    all_to_all x31, waiting for transfers between devices, copy_for_each(): return lax.all_to_all(copies, axis, split_axis=0, concat_axis=0, tiled=True)  281 us
    all_gather x1, waiting for transfers between devices, body(): lax.all_gather(mine_down, 'dp', axis=0, tiled=True)  181 us
    all_gather x1, waiting for transfers between devices, body(): lax.all_gather(mine_up, 'dp', axis=0, tiled=True)  181 us
    dot_general x13, matrix products, compute(): lax.dot_general(hidden, full_down, (((1,), (1,)), ((), ())), preferred_el...  168 us
    all_to_all x31, starting transfers between devices, copy_for_each(): return lax.all_to_all(copies, axis, split_axis=0, concat_axis=0, tiled=True)  144 us
    all_gather x1, waiting for transfers between devices, in_one_piece(): lax.all_gather(both, axis, axis=dim, tiled=True)  81.4 us
    ppermute x31, starting transfers between devices, passed_along(): return lax.ppermute(block, axis, route)  40.1 us
  transfers between devices with their start and end apart: 66, of which 66 were waited for; matrix products, arithmetic and copies ran while one was open for 3% of the time, Pallas kernels for 0%

commit v1 on v0

v1 whole, which is shorter than its diff:
```python
import functools

import jax
import jax.numpy as jnp
from jax import lax
from jax.experimental import pallas as pl
from jax.experimental.pallas import tpu as pltpu
from jax.sharding import PartitionSpec as P

MESH = pl.DeviceIdType.MESH
F32, BF16 = jnp.float32, jnp.bfloat16
M = 32
LAG_B, LAG_C = 1, 2
LOOK = 2


def wait_for(ref, sem):
    pltpu.make_async_copy(ref, ref, sem).wait()


def relay(
    n_section,
    n_tensor,
    up_ref,
    down_ref,
    gain_ref,
    mb_ref,
    out_ref,
    x_in,
    p_own,
    s_own,
    p_out,
    p_in,
    y_out,
    y_in,
    x_out,
    fin,
    x_recv,
    p_recv,
    y_recv,
    fin_recv,
    x_send,
    p_send,
    y_send,
    mb_send,
):
    s, t, d = lax.axis_index("section"), lax.axis_index("tensor"), lax.axis_index("dp")
    n_mb, tok = mb_ref.shape[0], mb_ref.shape[2]
    n_chunk, width = x_in.shape[0], x_in.shape[3]
    per_dp = tok // M
    half = n_tensor // 2
    features = n_tensor * width * 2
    hidden = down_ref.shape[1]
    cut = 1024

    def remote(src, dst, send, recv, where):
        return pltpu.make_async_remote_copy(src, dst, send, recv, device_id=where, device_id_type=MESH)

    def enter(b):
        for q in range(per_dp):
            c = (b * 2 + d) * per_dp + q
            src = mb_ref.at[b, :, pl.ds(q * M, M)]
            dst = x_in.at[c, pl.ds(lax.rem(t, half) * half, half)]
            for other in range(n_tensor):
                here = jnp.logical_and(t == other, d == t // half)

                @pl.when(here)
                def _():
                    pltpu.make_async_copy(src, dst, x_recv.at[c]).start()

                @pl.when(jnp.logical_not(here))
                def _():
                    remote(src, dst, mb_send.at[b], x_recv.at[c], (s, other, t // half)).start()

    def up_stage(c):
        wait_for(x_in.at[c], x_recv.at[c])
        squares = jnp.zeros((M, 1), F32)
        rows = []
        for j in range(n_tensor):
            values = x_in[c, j].astype(F32)
            squares = squares + jnp.sum(values * values, axis=1, keepdims=True)
            rows.append((values * gain_ref[:, j * width : (j + 1) * width]).astype(BF16))
        rows = jnp.concatenate(rows, axis=1)
        slot = lax.rem(c, LAG_B + 1)
        s_own[slot] = jnp.broadcast_to(squares, (M, 128))
        high = squares.astype(BF16)
        low = (squares - high.astype(F32)).astype(BF16)
        p_out[c, :, hidden : hidden + 64] = jnp.broadcast_to(high, (M, 64))
        p_out[c, :, hidden + 64 : hidden + 128] = jnp.broadcast_to(low, (M, 64))
        for lo, hi, end in ((0, cut, cut), (cut, hidden, hidden + 128)):
            terms = jnp.dot(rows, up_ref[:, lo:hi], preferred_element_type=F32)
            p_own[slot, :, lo:hi] = terms
            p_out[c, :, lo:hi] = terms.astype(BF16)
            remote(
                p_out.at[c, :, pl.ds(lo, end - lo)],
                p_in.at[c, :, pl.ds(lo, end - lo)],
                p_send.at[c],
                p_recv.at[c],
                (s, t, 1 - d),
            ).start()

    def down_stage(c):
        wait_for(p_in.at[c], p_recv.at[c])
        slot = lax.rem(c, LAG_B + 1)
        others = p_in[c, :, hidden : hidden + 1].astype(F32) + p_in[c, :, hidden + 64 : hidden + 65].astype(F32)
        scale = lax.rsqrt((s_own[slot, :, 0:1] + others) / features + 1e-05)
        v = (p_own[slot] + p_in[c, :, :hidden].astype(F32)) * scale
        act = (v / (1.0 + jnp.exp(-v))).astype(BF16)
        for step in (2, 1, 3, 0):
            to = lax.rem(t + step, n_tensor)
            y_out[c, step] = jnp.dot(act, down_ref[to], preferred_element_type=F32).astype(BF16)
            if step:
                remote(y_out.at[c, step], y_in.at[c, step - 1], y_send.at[c], y_recv.at[c], (s, to, d)).start()

    def sum_stage(c):
        wait_for(y_in.at[c], y_recv.at[c])
        total = x_in[c, t].astype(F32) + y_out[c, 0].astype(F32)
        for k in range(n_tensor - 1):
            total = total + y_in[c, k].astype(F32)
        x_out[c] = total.astype(BF16)

        @pl.when(s < n_section - 1)
        def _():
            for other in range(n_tensor):
                remote(x_out.at[c], x_in.at[c, t], x_send.at[c], x_recv.at[c], (s + 1, other, d)).start()

        @pl.when(s == n_section - 1)
        def _():
            b, to_d, q = final_place(c)
            to_t = half * d + t // half
            dst = fin.at[lax.rem(t, half), pl.ds(q * M, M)]
            here = at_home(b, to_d, to_t)

            @pl.when(here)
            def _():
                pltpu.make_async_copy(x_out.at[c], dst, fin_recv).start()

            @pl.when(jnp.logical_not(here))
            def _():
                remote(x_out.at[c], dst, x_send.at[c], fin_recv, (b, to_t, to_d)).start()

    def final_place(c):
        return c // (2 * per_dp), lax.rem(c // per_dp, 2), lax.rem(c, per_dp)

    def at_home(b, to_d, to_t):
        return jnp.logical_and(b == s, jnp.logical_and(to_d == d, to_t == t))

    @pl.when(s == 0)
    def _():
        for b in range(LOOK):
            enter(b)

    def tick(k, carry):
        ahead = k // (2 * per_dp) + LOOK

        @pl.when(jnp.logical_and(s == 0, jnp.logical_and(lax.rem(k, 2 * per_dp) == 0, ahead < n_mb)))
        def _():
            enter(ahead)

        @pl.when(k < n_chunk)
        def _():
            up_stage(k)

        @pl.when(jnp.logical_and(k >= LAG_B, k < n_chunk + LAG_B))
        def _():
            down_stage(k - LAG_B)

        @pl.when(k >= LAG_C)
        def _():
            sum_stage(k - LAG_C)

        return carry

    lax.fori_loop(0, n_chunk + LAG_C, tick, 0)

    def drain(c, carry):
        wait_for(p_out.at[c], p_send.at[c])
        wait_for(y_in.at[c], y_send.at[c])

        @pl.when(s < n_section - 1)
        def _():
            wait_for(x_in.at[c], x_send.at[c])

        b, to_d, q = final_place(c)
        sent = jnp.logical_not(at_home(b, to_d, half * d + t // half))

        @pl.when(jnp.logical_and(s == n_section - 1, sent))
        def _():
            wait_for(x_out.at[c], x_send.at[c])

        return carry

    lax.fori_loop(0, n_chunk, drain, 0)

    @pl.when(s == 0)
    def _():
        def drained(b, carry):
            mine = d == t // half

            @pl.when(mine)
            def _():
                wait_for(x_in.at[pl.ds(0, (n_tensor - 1) * per_dp), pl.ds(0, half)], mb_send.at[b])

            @pl.when(jnp.logical_not(mine))
            def _():
                wait_for(x_in.at[pl.ds(0, n_tensor * per_dp), pl.ds(0, half)], mb_send.at[b])

            return carry

        lax.fori_loop(0, n_mb, drained, 0)

    wait_for(fin, fin_recv)
    for k in range(half):
        out_ref[0, :, k * width : (k + 1) * width] = fin[k]


def pipelined(mesh, up, down, gain, entering):
    n_section, n_tensor = mesh.shape["section"], mesh.shape["tensor"]
    n_mb, half, tok, width = entering.shape
    n_chunk = n_mb * 2 * tok // M
    hidden = up.shape[1]
    dma = pltpu.SemaphoreType.DMA
    return pl.pallas_call(
        functools.partial(relay, n_section, n_tensor),
        out_shape=jax.ShapeDtypeStruct((1, tok, half * width), BF16),
        in_specs=[pl.BlockSpec(memory_space=pltpu.VMEM)] * 4,
        out_specs=pl.BlockSpec(memory_space=pltpu.VMEM),
        scratch_shapes=[
            pltpu.VMEM((n_chunk, n_tensor, M, width), BF16),
            pltpu.VMEM((LAG_B + 1, M, hidden), F32),
            pltpu.VMEM((LAG_B + 1, M, 128), F32),
            pltpu.VMEM((n_chunk, M, hidden + 128), BF16),
            pltpu.VMEM((n_chunk, M, hidden + 128), BF16),
            pltpu.VMEM((n_chunk, n_tensor, M, width), BF16),
            pltpu.VMEM((n_chunk, n_tensor - 1, M, width), BF16),
            pltpu.VMEM((n_chunk, M, width), BF16),
            pltpu.VMEM((half, tok, width), BF16),
            dma((n_chunk,)),
            dma((n_chunk,)),
            dma((n_chunk,)),
            dma,
            dma((n_chunk,)),
            dma((n_chunk,)),
            dma((n_chunk,)),
            dma((n_mb,)),
        ],
        compiler_params=pltpu.CompilerParams(has_side_effects=True, vmem_limit_bytes=60 * 1024 * 1024),
    )(up, down, gain, entering)


def sent_together(arrays, axis, split_dim, concat_dim, along):
    widths = [a.shape[along] for a in arrays]
    both = jnp.concatenate(arrays, axis=along)
    filled = lax.all_to_all(both, axis, split_axis=split_dim, concat_axis=concat_dim, tiled=True)
    return tuple(jnp.split(filled, [sum(widths[:k]) for k in range(1, len(widths))], axis=along))


def in_one_piece(arrays, axis, dim, along):
    ends, at = ([], 0)
    for a in arrays[:-1]:
        at += a.shape[along]
        ends.append(at)
    both = jnp.concatenate(arrays, axis=along)
    return tuple(jnp.split(lax.all_gather(both, axis, axis=dim, tiled=True), ends, axis=along))


def body(
    mesh,
    section_up,
    section_down,
    backup_up,
    backup_down,
    norm_gain,
    micro_batches,
    failed_section,
    live_batches,
):
    n_tensor = lax.axis_size("tensor")
    pieces = sent_together((backup_up, backup_down), "tensor", 4, 2, 0)
    gathered = in_one_piece((pieces[0], pieces[1]), "section", 1, 0)
    rows, block_width = section_up.shape[1], section_up.shape[2]
    rebuilt_up = gathered[0].reshape(-1, block_width)
    rebuilt_down = gathered[1].reshape(-1, block_width)
    is_failed = lax.axis_index("section") == failed_section[0] % lax.axis_size("section")
    mine_up = jnp.where(is_failed, rebuilt_up, section_up[0])
    mine_down = jnp.where(is_failed, rebuilt_down, section_down[0])
    mine_down = mine_down.reshape(n_tensor, rows // n_tensor, block_width).swapaxes(1, 2)
    gain = lax.dynamic_slice_in_dim(norm_gain, lax.axis_index("dp") * rows, rows, 1)
    batch_count, tok_rows, share = micro_batches.shape
    live_count = batch_count // 2 + live_batches[0] % (batch_count - batch_count // 2 + 1)
    is_live = jnp.arange(batch_count, dtype=jnp.int32)[:, None, None, None] < live_count
    width = rows // n_tensor
    entering = micro_batches.reshape(batch_count, tok_rows, share // width, width).swapaxes(1, 2)
    entering = jnp.where(is_live, entering, jnp.zeros_like(entering))
    return pipelined(mesh, mine_up, mine_down, gain, entering)


def solution(mesh):
    placed = (
        P("section", "dp", "tensor"),
        P("section", "dp", "tensor"),
        P("dp", "section", "tensor", None, None),
        P("dp", "section", "tensor", None, None),
        P("section", None),
        P(None, "dp", "tensor"),
        P(),
        P(),
    )
    return jax.shard_map(
        functools.partial(body, mesh),
        mesh=mesh,
        in_specs=placed,
        out_specs=P("section", "dp", "tensor"),
        check_vma=False,
    )
```

time: 1670 us -> 627 us (0.38)
  waiting for transfers between devices: 1120 us -> 69.7 us
  Pallas kernels: 0 us -> 434 us
  starting transfers between devices: 184 us -> 0.01 us
  matrix products: 168 us -> 0 us
  other arithmetic: 61.6 us -> 19.7 us
  blocking collectives: 39.4 us -> 16.3 us
    pallas_call x0 -> x1, Pallas kernels: none -> 434 us  [pipelined(): pl.pallas_call(functools.partial(relay, n_section, n_tensor), out_shape=j...]
    ppermute x31 -> x0, waiting for transfers between devices: 388 us -> none  [passed_along(): return lax.ppermute(block, axis, route)]
    all_gather x3 -> x0, waiting for transfers between devices: 368 us -> none  [the longest x1 181 us: body(): lax.all_gather(mine_down, 'dp', axis=0, tiled=True)]
    all_to_all x31 -> x0, waiting for transfers between devices: 281 us -> none  [copy_for_each(): return lax.all_to_all(copies, axis, split_axis=0, concat_axis=0, tiled=True)]
    dot_general x13 -> x0, matrix products: 168 us -> none  [compute(): lax.dot_general(hidden, full_down, (((1,), (1,)), ((), ())), preferred_el...]
    all_to_all x31 -> x0, starting transfers between devices: 144 us -> none  [copy_for_each(): return lax.all_to_all(copies, axis, split_axis=0, concat_axis=0, tiled=True)]
    ppermute x31 -> x0, starting transfers between devices: 40.1 us -> none  [passed_along(): return lax.ppermute(block, axis, route)]
    select_n x32 -> x1, other arithmetic: 39.4 us -> 1.18 us  [body(): entering = jnp.where(is_live, entering, jnp.zeros_like(entering))]
  transfers between devices with their start and end apart: 66 -> 1, of which waited for: 66 -> 1; matrix products, arithmetic and copies ran while one was open for 3% -> 2% of each run, Pallas kernels for 0% -> 0%
where the time goes in v1:
time: 627 us; the launch traced here: 626 us
  Pallas kernels  434 us (69%)
  local copies, waits for them, and re-layouts  70.6 us (11%)
  waiting for transfers between devices  69.7 us (11%)
  other arithmetic  19.7 us (3%)
  blocking collectives  16.3 us (3%)
  between operations  14.8 us (2%)
    pallas_call x1, Pallas kernels, pipelined(): pl.pallas_call(functools.partial(relay, n_section, n_tensor), out_shape=j...  434 us
    all_gather x1, waiting for transfers between devices, in_one_piece(): lax.all_gather(both, axis, axis=dim, tiled=True)  69.6 us
    split x3, local copies, waits for them, and re-layouts, in_one_piece(): jnp.split(lax.all_gather(both, axis, axis=dim, tiled=True), ends, axis=al...  25.1 us
    all_to_all x1, blocking collectives, sent_together(): lax.all_to_all(both, axis, split_axis=split_dim, concat_axis=concat_dim,...  16.3 us
  transfers between devices with their start and end apart: 1, of which 1 were waited for; matrix products, arithmetic and copies ran while one was open for 2% of the time, Pallas kernels for 0%

profile of v1, /device:TPU:63, one launch (start us, length us, event | category | flops | bytes accessed | tf_op | source)
XLA Modules:
  0.0 625.5 jit_solution(246869857902134540)
XLA Ops:
  6.5 0.0 copy-start
  6.5 0.0 all-gather.2.cloned.1.call-start
  6.5 1.3 pad_maximum_fusion
  7.8 6.1 copy.28
  13.9 5.2 reshape.24
  19.0 16.3 %all_to_all.15 = bf16[4,2,57344]{2,1,0:T(2,128)(2,1)S(1)} all-to-all(bf16[4,2,57344]{2,1,0:T(2,128)(2,1)S(1)} %reshape.24), channel_id=1, replica_groups=mesh['section'=16,'tensor'=4,'dp'=2] {'tensor'}, dimensions={0} | all-to-all | bytes 1835008 | tf_op jit(solution)/shard_map/all_to_all | solution.py:254
  35.3 3.2 reshape.25
  38.6 8.6 %copy.36 = bf16[2,1,1,32,4,1792]{5,4,3,0,2,1:T(4,128)(2,1)S(1)} copy(bf16[2,1,1,32,4,1792]{3,0,5,4,2,1:T(2,128)(2,1)} %bitcast.32) | data formatting | bytes 1835008 | tf_op jit(solution)/shard_map/all_to_all | solution.py:254
  47.1 0.2 slice_bitcast_fusion
  47.3 0.2 slice_bitcast_fusion.1
  47.5 1.6 pad_maximum_fusion.1
  49.1 0.0 all-gather.2.cloned.1.call-update
  50.5 0.0 copy-start.2
  50.5 10.1 %copy.34 = bf16[4,512,1792]{1,2,0:T(8,128)(2,1)} copy(bf16[4,512,1792]{2,1,0:T(8,128)(2,1)} %bitcast.33) | data formatting | bytes 14680064 | tf_op jit(solution)/shard_map/squeeze | solution.py:286
  60.6 0.0 copy-done
  60.6 0.6 constant_dynamic-slice_fusion.gain_ref
  61.2 0.0 copy-done.2
  61.2 1.2 fusion.mb_ref
  62.4 69.6 %all-gather.2.cloned.1.call-done = bf16[2,16,4,32,1792]{4,2,3,1,0:T(4,128)(2,1)} async-done(((bf16[2,1,4,32,1792]{4,2,3,1,0:T(4,128)(2,1)}), bf16[2,16,4,32,1792]{4,2,3,1,0:T(4,128)(2,1)}) %all-gather.2.cloned.1.call-update) | async-done | bytes 14680080 | tf_op jit(solution)/shard_map/all_gather | solution.py:264
  132.0 13.0 %fusion.1 = (bf16[1,16,4,32,1792]{4,2,3,1,0:T(4,128)(2,1)S(1)}, bf16[1,16,4,32,1792]{4,2,3,1,0:T(4,128)(2,1)}) fusion(bf16[2,16,4,32,1792]{4,2,3,1,0:T(4,128)(2,1)} %all-gather.2.cloned.1.call-done), kind=kLoop, calls=%fused_computation.10 | loop fusion | bytes 29360128 | tf_op jit(solution)/shard_map/split | solution.py:264
  145.0 7.6 %copy.31 = bf16[1,16,4,32,1792]{4,3,2,1,0:T(8,128)(2,1)} copy(bf16[1,16,4,32,1792]{4,2,3,1,0:T(4,128)(2,1)} %get-tuple-element.6) | data formatting | bytes 14680064 | tf_op jit(solution)/shard_map/split | solution.py:264
  152.6 4.5 copy.32
  157.1 10.0 %copy.33 = bf16[4,512,1792]{1,2,0:T(8,128)(2,1)} copy(bf16[4,512,1792]{2,1,0:T(8,128)(2,1)} %bitcast.30) | data formatting | bytes 14680064 | tf_op jit(solution)/shard_map/reshape | solution.py:283
  167.1 8.9 %bitcast_select_fusion.up_ref = bf16[2048,1792]{1,0:T(8,128)(2,1)} fusion(bf16[1,2048,1792]{2,1,0:T(8,128)(2,1)} %param.8, bf16[1,16,4,32,1792]{4,3,2,1,0:T(8,128)(2,1)} %copy.31, pred[]{:T(512)S(6)} %eq.6), kind=kLoop, calls=%fused_computation | loop fusion | flops 3670016 | bytes 22020096 | tf_op jit(solution)/shard_map/jit(_where)/select_n | solution.py:285
  175.9 0.0 copy-start.1
  175.9 6.8 %select_bitcast_fusion.down_ref = bf16[4,1792,512]{2,1,0:T(8,128)(2,1)} fusion(bf16[4,512,1792]{1,2,0:T(8,128)(2,1)} %copy.33, bf16[4,512,1792]{1,2,0:T(8,128)(2,1)} %copy.34, pred[]{:T(512)S(6)} %eq.6), kind=kLoop, calls=%fused_computation.1 | loop fusion | flops 3670016 | bytes 22020096 | tf_op jit(solution)/shard_map/transpose | solution.py:287
  182.7 434.4 %shard_map.82 = bf16[1,32,1024]{2,1,0:T(8,128)(2,1)} custom-call(bf16[2048,1792]{1,0:T(8,128)(2,1)} %bitcast_select_fusion.up_ref, bf16[4,1792,512]{2,1,0:T(8,128)(2,1)} %select_bitcast_fusion.down_ref, f32[1,2048]{1,0:T(1,128)} %constant_dynamic-slice_fusion.gain_ref, bf16[16,2,32,512]{3,2,1,0:T(8,128)(2,1)} %fusion.mb_ref), custom_call_target="tpu_custom_call" | custom-call | tf_op jit(solution)/shard_map/pallas_call | solution.py:223
  617.2 1.5 copy.42
  618.7 0.0 copy-done.1
  (1 shorter events, 0.0 us)
Async XLA Ops:
  6.5 54.0 %copy-start = (f32[1,4096]{1,0:T(1,128)S(1)}, f32[1,4096]{1,0:T(1,128)}, u32[]{:S(2)}) copy-start(f32[1,4096]{1,0:T(1,128)} %param.12) | copy-start | bytes 49156
  6.5 125.5 %all-gather.2.cloned.1.call-start = ((), (), s32[]{:S(2)}) async-start(), calls=%async_computation.1 | async-start | bytes 15597568 | tf_op jit(solution)/shard_map/all_gather | solution.py:264
  50.5 10.7 %copy-start.2 = (bf16[16,32,1024]{2,1,0:T(8,128)(2,1)S(1)}, bf16[16,32,1024]{2,1,0:T(8,128)(2,1)}, u32[]{:S(2)}) copy-start(bf16[16,32,1024]{2,1,0:T(8,128)(2,1)} %param.13) | copy-start | bytes 3145732
  175.9 442.7 %copy-start.1 = (f32[1,4096]{1,0:T(1,128)S(1)}, f32[1,4096]{1,0:T(1,128)}, u32[]{:S(2)}) copy-start(f32[1,4096]{1,0:T(1,128)} %param.12) | copy-start | bytes 49156
Sparse Core Ops, SparseCore 0:
  49.2 82.6 all-gather.1
